TPU v7x, 32 devices: a whole 2x2x4 slice. The times are simulated.
32 devices in a mesh: seq: 8 (over z, y), head: 4 (over x, core).
Axes of the slice: x: 2, y: 2, z: 4, core: 2. Of those that a mesh axis runs over, the one named last changes fastest.
Arguments:
- residual: bfloat16 [4096, 3072], P('seq', 'head'), may hold values from -6 to 6
- q_self: bfloat16 [4096, 3072], P('seq', 'head'), may hold values from -6 to 6
- k_self: bfloat16 [4096, 3072], P('seq', 'head'), may hold values from -6 to 6
- v_self: bfloat16 [4096, 3072], P('seq', 'head'), may hold values from -6 to 6
- w_out: bfloat16 [3072, 3072], P('head'), may hold values from -0.109375 to 0.109375
- norm_gain: float32 [3072], replicated, may hold values from 0.5 to 1.5
- w_query: bfloat16 [3072, 3072], P('seq', 'head')
- w_cache: bfloat16 [3072, 2048], P('seq', 'head')
- block_doc: int32 [8], replicated, may hold values from 0 to 2, never falling along the last dimension, each value on 1 to 4 neighbouring positions
- tail_len: int32 [8], replicated, may hold values from 1 to 512
Outputs:
- hidden: bfloat16 [4096, 3072], P('seq', 'head')
- cross_context: bfloat16 [4096, 3072], P('seq', 'head')
Inputs may be any that keep to these rules, and one draw needn't show every extreme that they name: block_doc never falls along the blocks; each document covers 1 to 4 consecutive blocks, and some document covers exactly 4. `tail_len`: read only for the last block of a document.
All inputs are finite; a program needn't handle non-finite values.
Results may differ from a plain program's by a relative error of at most 0.0078.
Values may be sent and summed in bfloat16 or wider, within the bound.
No kernel may reach another device: no remote copies, remote signals or barrier semaphores. Data moves between devices by JAX's collectives and lax.ppermute only.
A program may use at most 128 MiB of HBM per device.

v0:
```python
import math
import jax
import jax.numpy as jnp
from jax import lax
from jax.sharding import PartitionSpec as P

D = 3072
HEAD_DIM = 128
WINDOW = 2048
DOC_MAX = 2560
WIN_BLOCKS = 4
DOC_BLOCKS = 5
EPSILON = 1e-06


def passed_along(block, axis, distance):
    devices = range(lax.axis_size(axis))
    route = [(i - distance, i) for i in devices if i - distance in devices]
    return lax.ppermute(block, axis, route)


def block_valid(block_doc, tail_len, tok_rows):
    following = jnp.concatenate([block_doc[1:], jnp.full((1,), -1, jnp.int32)])
    closing = following != block_doc
    within = jnp.arange(tok_rows, dtype=jnp.int32)
    return jnp.logical_or(jnp.logical_not(closing)[:, None], within[None, :] < tail_len[:, None])


def permitted(query_block, key_blocks, block_doc, valid_tokens, tok_rows, reach_tokens):
    inside = key_blocks >= 0
    safe_blocks = jnp.maximum(key_blocks, 0)
    own_doc = jnp.take(block_doc, query_block)
    same_doc = jnp.logical_and(inside, jnp.take(block_doc, safe_blocks) == own_doc)
    live_keys = jnp.logical_and(same_doc[:, None], jnp.take(valid_tokens, safe_blocks, axis=0))
    within = jnp.arange(tok_rows, dtype=jnp.int32)
    query_pos = query_block * tok_rows + within
    key_pos = (key_blocks[:, None] * tok_rows + within[None, :]).reshape(-1)
    distance = query_pos[:, None] - key_pos[None, :]
    near = jnp.logical_and(distance >= 0, distance < reach_tokens)
    return jnp.logical_and(near, live_keys.reshape(-1)[None, :])


def attend(queries, keys, values, allowed):
    row_count, head_count, head_dim = queries.shape
    group_size = head_count // keys.shape[1]
    scaling = 1.0 / math.sqrt(head_dim)

    def one_head(head_index):
        query_head = lax.dynamic_index_in_dim(queries, head_index, 1, keepdims=False)
        key_head = lax.dynamic_index_in_dim(keys, head_index // group_size, 1, keepdims=False)
        value_head = lax.dynamic_index_in_dim(values, head_index // group_size, 1, keepdims=False)
        scores = (
            lax.dot_general(
                query_head, key_head, (((1,), (1,)), ((), ())), preferred_element_type=jnp.float32
            )
            * scaling
        )
        scores = jnp.where(allowed, scores, -1e30)
        row_peak = jnp.max(scores, axis=1, keepdims=True)
        weights = jnp.exp(scores - row_peak)
        row_total = jnp.sum(weights, axis=1, keepdims=True)
        blended = jnp.dot(
            weights.astype(jnp.bfloat16), value_head, preferred_element_type=jnp.float32
        )
        return (blended / row_total).astype(jnp.bfloat16)

    per_head = lax.map(one_head, jnp.arange(head_count, dtype=jnp.int32))
    return jnp.transpose(per_head, (1, 0, 2)).reshape(row_count, head_count * head_dim)


def local(
    residual, q_self, k_self, v_self, w_out, norm_gain, w_query, w_cache, block_doc, tail_len
):
    tok_rows = residual.shape[0]
    local_heads = q_self.shape[1] // HEAD_DIM
    local_kv = w_cache.shape[1] // (2 * HEAD_DIM)
    query_width = local_heads * HEAD_DIM
    block_index = lax.axis_index("seq")
    valid_tokens = block_valid(block_doc, tail_len, tok_rows)
    stacked = jnp.concatenate([k_self, v_self], axis=1)
    earlier = []
    for offset in range(WIN_BLOCKS, 0, -1):
        earlier.append(passed_along(stacked, "seq", offset))
    window = jnp.concatenate(earlier + [stacked], axis=0)
    key_blocks = block_index - WIN_BLOCKS + jnp.arange(WIN_BLOCKS + 1, dtype=jnp.int32)
    allowed = permitted(block_index, key_blocks, block_doc, valid_tokens, tok_rows, WINDOW)
    context = attend(
        q_self.reshape(tok_rows, local_heads, HEAD_DIM),
        window[:, :query_width].reshape(-1, local_heads, HEAD_DIM),
        window[:, query_width:].reshape(-1, local_heads, HEAD_DIM),
        allowed,
    )
    partial_terms = jnp.dot(context, w_out, preferred_element_type=jnp.float32)
    own_columns = residual.shape[1]
    column_share = lax.psum_scatter(partial_terms, "head", scatter_dimension=1, tiled=True)
    hidden = (residual.astype(jnp.float32) + column_share).astype(jnp.bfloat16)
    wide = hidden.astype(jnp.float32)
    square_total = lax.psum(jnp.sum(wide * wide, axis=1), "head")
    inverse_rms = lax.rsqrt(square_total / D + EPSILON)
    gain_share = lax.dynamic_slice_in_dim(
        norm_gain, lax.axis_index("head") * own_columns, own_columns, 0
    )
    normed_share = (wide * inverse_rms[:, None] * gain_share).astype(jnp.bfloat16)
    normed = lax.all_gather(normed_share, "head", axis=1, tiled=True)
    query_sum = jnp.dot(
        normed,
        lax.all_gather(w_query, "seq", axis=0, tiled=True),
        preferred_element_type=jnp.float32,
    )
    cache_sum = jnp.dot(
        normed,
        lax.all_gather(w_cache, "seq", axis=0, tiled=True),
        preferred_element_type=jnp.float32,
    )
    cross_queries = query_sum.astype(jnp.bfloat16)
    cache_rows = cache_sum.astype(jnp.bfloat16)
    earlier_cache = []
    for offset in range(DOC_BLOCKS - 1, 0, -1):
        earlier_cache.append(passed_along(cache_rows, "seq", offset))
    history = jnp.concatenate(earlier_cache + [cache_rows], axis=0)
    doc_key_blocks = block_index - DOC_BLOCKS + 1 + jnp.arange(DOC_BLOCKS, dtype=jnp.int32)
    doc_allowed = permitted(block_index, doc_key_blocks, block_doc, valid_tokens, tok_rows, DOC_MAX)
    kv_width = local_kv * HEAD_DIM
    cross_context = attend(
        cross_queries.reshape(tok_rows, local_heads, HEAD_DIM),
        history[:, :kv_width].reshape(-1, local_kv, HEAD_DIM),
        history[:, kv_width:].reshape(-1, local_kv, HEAD_DIM),
        doc_allowed,
    )
    return (hidden, cross_context)


def solution(mesh):
    in_specs = (
        P("seq", "head"),
        P("seq", "head"),
        P("seq", "head"),
        P("seq", "head"),
        P("head", None),
        P(),
        P("seq", "head"),
        P("seq", "head"),
        P(),
        P(),
    )
    out_specs = (P("seq", "head"), P("seq", "head"))
    return jax.shard_map(local, mesh=mesh, in_specs=in_specs, out_specs=out_specs, check_vma=False)
```

profile of v0, /device:TPU:17, one launch (start us, length us, event | category | flops | bytes accessed | tf_op | source)
XLA Modules:
  0.0 584.7 jit_solution(10366672590483666135)
XLA Ops:
  8.1 1.4 copy.14
  9.5 1.4 copy.15
  11.0 1.3 collective-permute-start
  12.3 4.2 collective-permute-start.1
  16.5 1.9 collective-permute-start.2
  18.4 1.9 collective-permute-start.3
  23.3 2.3 copy.13
  25.6 23.7 %collective-permute-done = bf16[512,1536]{0,1:T(8,128)(2,1)} collective-permute-done((bf16[512,1536]{0,1:T(8,128)(2,1)S(1)}, bf16[512,1536]{0,1:T(8,128)(2,1)}, u32[]{:S(2)}, u32[]{:S(2)}) %collective-permute-start) | collective-permute-done | bytes 1572896 | tf_op jit(solution)/shard_map/ppermute | solution.py:19
  49.2 1.5 constant_dynamic-update-slice_fusion.6
  50.7 33.1 %collective-permute-done.1 = bf16[512,1536]{0,1:T(8,128)(2,1)} collective-permute-done((bf16[512,1536]{0,1:T(8,128)(2,1)S(1)}, bf16[512,1536]{0,1:T(8,128)(2,1)}, u32[]{:S(2)}, u32[]{:S(2)}) %collective-permute-start.1) | collective-permute-done | bytes 1572896 | tf_op jit(solution)/shard_map/ppermute | solution.py:19
  83.9 1.5 constant_dynamic-update-slice_fusion.5
  85.4 66.0 %collective-permute-done.2 = bf16[512,1536]{0,1:T(8,128)(2,1)} collective-permute-done((bf16[512,1536]{0,1:T(8,128)(2,1)S(1)}, bf16[512,1536]{0,1:T(8,128)(2,1)}, u32[]{:S(2)}, u32[]{:S(2)}) %collective-permute-start.2) | collective-permute-done | bytes 1572896 | tf_op jit(solution)/shard_map/ppermute | solution.py:19
  151.4 1.5 constant_dynamic-update-slice_fusion.4
  152.9 66.9 %collective-permute-done.3 = bf16[512,1536]{0,1:T(8,128)(2,1)} collective-permute-done((bf16[512,1536]{0,1:T(8,128)(2,1)S(1)}, bf16[512,1536]{0,1:T(8,128)(2,1)}, u32[]{:S(2)}, u32[]{:S(2)}) %collective-permute-start.3) | collective-permute-done | bytes 1572896 | tf_op jit(solution)/shard_map/ppermute | solution.py:19
  219.8 1.5 constant_dynamic-update-slice_fusion.3
  221.4 3.4 fusion.60
  224.8 53.3 %while.27 = (s32[]{:T(128)}, bf16[6,512,128]{1,2,0:T(8,128)(2,1)S(1)}, s32[6]{0:T(128)S(1)}, bf16[512,6,128]{0,2,1:T(8,128)(2,1)}, bf16[2560,6,128]{0,2,1:T(8,12...) while((s32[]{:T(128)}, ...), condition=%wide.region_3.6_spmd.clone, body=%wide.region_0.5_spmd.clone.sunk | while | flops 686947328 | bytes 17852076 | solution.py:67
  227.5 3.2 fusion.80
  231.6 2.0 fusion.82
  236.4 3.2 fusion.80
  239.6 0.8 fusion.81
  240.4 2.0 fusion.82
  245.3 3.2 fusion.80
  249.3 2.0 fusion.82
  254.1 3.2 fusion.80
  257.3 0.8 fusion.81
  258.2 2.0 fusion.82
  263.0 3.2 fusion.80
  267.1 2.0 fusion.82
  271.9 3.2 fusion.80
  275.1 0.8 fusion.81
  275.9 2.0 fusion.82
  278.1 6.9 %fusion.61 = f32[512,3072]{1,0:T(8,128)} fusion(bf16[512,768]{0,1:T(8,128)(2,1)S(1)} %bitcast.88, bf16[768,3072]{1,0:T(8,128)(2,1)} %param.22), kind=kOutput, calls=%fused_computation.87 | convolution fusion | flops 2415919104 | bytes 11796480 | tf_op jit(solution)/shard_map/dot_general | solution.py:93
  286.4 55.4 %reduce-scatter.2.cloned.1.call-done = f32[512,768]{1,0:T(8,128)} async-done(((f32[512,3072]{1,0:T(8,128)}), f32[512,768]{1,0:T(8,128)}) %reduce-scatter.2.cloned.1.call-update) | async-done | bytes 1572880 | tf_op jit(solution)/shard_map/reduce_scatter | solution.py:95
  341.8 1.7 fusion.52
  343.5 5.9 %psum.7 = f32[512]{0:T(512)S(1)} all-reduce(f32[512]{0:T(512)S(1)} %get-tuple-element.300), channel_id=1, replica_groups=mesh['seq'=8,'head'=4] {'head'}, use_global_device_ids=true, to_apply=%region_6.9 | all-reduce | flops 512 | bytes 4096 | tf_op jit(solution)/shard_map/psum | solution.py:98
  349.4 1.1 fusion.54
  351.2 29.0 %all-gather.4.cloned.1.call-done = bf16[512,3072]{1,0:T(8,128)(2,1)} async-done(((bf16[512,768]{1,0:T(8,128)(2,1)}), bf16[512,3072]{1,0:T(8,128)(2,1)}) %all-gather.4.cloned.1.call-update) | async-done | bytes 3145744 | tf_op jit(solution)/shard_map/all_gather | solution.py:104
  380.1 4.6 convolution_convert_fusion.1
  384.8 1.3 collective-permute-start.4
  386.1 4.0 collective-permute-start.5
  390.1 1.9 collective-permute-start.6
  392.0 2.1 collective-permute-start.7
  394.1 102.8 %all-gather.6.cloned.1.call-done = bf16[3072,768]{1,0:T(8,128)(2,1)} async-done(((bf16[384,768]{1,0:T(8,128)(2,1)}), bf16[3072,768]{1,0:T(8,128)(2,1)}) %all-gather.6.cloned.1.call-update) | async-done | bytes 4718608 | tf_op jit(solution)/shard_map/all_gather | solution.py:107
  496.9 5.9 %convolution_convert_fusion = bf16[512,768]{1,0:T(8,128)(2,1)S(1)} fusion(bf16[512,3072]{1,0:T(8,128)(2,1)} %all-gather.4.cloned.1.call-done, bf16[3072,768]{1,0:T(8,128)(2,1)} %all-gather.6.cloned.1.call-done), kind=kOutput, calls=%fused_computation.55 | convolution fusion | flops 2416312320 | bytes 8650752 | tf_op jit(solution)/shard_map/dot_general | solution.py:105
  503.1 1.1 constant_dynamic-update-slice_fusion.11
  504.2 1.1 constant_dynamic-update-slice_fusion.10
  505.3 10.2 %collective-permute-done.7 = bf16[512,512]{1,0:T(8,128)(2,1)S(1)} collective-permute-done((bf16[512,512]{1,0:T(8,128)(2,1)S(1)}, bf16[512,512]{1,0:T(8,128)(2,1)S(1)}, u32[]{:S(2)}, u32[]{:S(2)}) %collective-permute-start.7) | collective-permute-done | bytes 524320 | tf_op jit(solution)/shard_map/ppermute | solution.py:19
  516.2 1.2 copy.39
  517.4 58.5 %while.28 = (s32[]{:T(128)}, bf16[6,512,128]{1,2,0:T(8,128)(2,1)S(1)}, s32[6]{0:T(128)S(1)}, bf16[512,6,128]{0,2,1:T(8,128)(2,1)S(1)}, bf16[2560,2,128]{2,0,1:T(...) while((s32[]{:T(128)}, ...), condition=%wide.region_10.13_spmd.clone, body=%wide.region_7.12_spmd.clone.sunk | while | flops 686947328 | bytes 17853756 | solution.py:67
  521.9 3.3 fusion.85
  525.3 0.8 fusion.86
  526.1 0.9 fusion.87
  531.7 3.3 fusion.85
  535.9 0.9 fusion.87
  541.4 3.3 fusion.85
  545.6 0.9 fusion.87
  551.2 3.3 fusion.85
  555.4 0.9 fusion.87
  560.9 3.3 fusion.85
  565.1 0.9 fusion.87
  570.7 3.3 fusion.85
  574.9 0.9 fusion.87
  575.9 1.2 copy.25
  (93 shorter events, 21.3 us)
Async XLA Ops:
  8.0 333.8 %reduce-scatter.2.cloned.1.call-start = ((), (), s32[]{:S(2)}) async-start(), calls=%async_computation.1 | async-start | bytes 7864320 | tf_op jit(solution)/shard_map/reduce_scatter | solution.py:95
  8.0 12.3 %copy-start = (s32[8]{0:T(128)S(1)}, s32[8]{0:T(128)}, u32[]{:S(2)}) copy-start(s32[8]{0:T(128)} %param.26) | copy-start | bytes 100
  8.1 14.4 %copy-start.3 = (s32[8]{0:T(128)S(1)}, s32[8]{0:T(128)}, u32[]{:S(2)}) copy-start(s32[8]{0:T(128)} %param.27) | copy-start | bytes 100
  11.0 38.2 %collective-permute-start = (bf16[512,1536]{0,1:T(8,128)(2,1)S(1)}, bf16[512,1536]{0,1:T(8,128)(2,1)}, u32[]{:S(2)}, u32[]{:S(2)}) collective-permute-start(bf16[512,1536]{0,1:T(8,128)(2,1)S(1)} %pad_maximum_fusion), channel_id=1, source_target_pairs={{0,16},{4,20},{8,24},{12,28},{1,17},{5,21},{9,25},{13,29},{2,18},{... | collective-permute-start | bytes 4718600 | tf_op jit(solution)/shard_map/ppermute | solution.py:19
  12.3 71.6 %collective-permute-start.1 = (bf16[512,1536]{0,1:T(8,128)(2,1)S(1)}, bf16[512,1536]{0,1:T(8,128)(2,1)}, u32[]{:S(2)}, u32[]{:S(2)}) collective-permute-start(bf16[512,1536]{0,1:T(8,128)(2,1)S(1)} %pad_maximum_fusion), channel_id=1, source_target_pairs={{0,12},{4,16},{8,20},{12,24},{16,28},{1,13},{5,17},{9,21},{13,25},... | collective-permute-start | bytes 4718600 | tf_op jit(solution)/shard_map/ppermute | solution.py:19
  16.5 134.9 %collective-permute-start.2 = (bf16[512,1536]{0,1:T(8,128)(2,1)S(1)}, bf16[512,1536]{0,1:T(8,128)(2,1)}, u32[]{:S(2)}, u32[]{:S(2)}) collective-permute-start(bf16[512,1536]{0,1:T(8,128)(2,1)S(1)} %pad_maximum_fusion), channel_id=1, source_target_pairs={{0,8},{4,12},{8,16},{12,20},{16,24},{20,28},{1,9},{5,13},{9,17},{1... | collective-permute-start | bytes 4718600 | tf_op jit(solution)/shard_map/ppermute | solution.py:19
  18.4 201.3 %collective-permute-start.3 = (bf16[512,1536]{0,1:T(8,128)(2,1)S(1)}, bf16[512,1536]{0,1:T(8,128)(2,1)}, u32[]{:S(2)}, u32[]{:S(2)}) collective-permute-start(bf16[512,1536]{0,1:T(8,128)(2,1)S(1)} %pad_maximum_fusion), channel_id=1, source_target_pairs={{0,4},{4,8},{8,12},{12,16},{16,20},{20,24},{24,28},{1,5},{5,9},{9,... | collective-permute-start | bytes 4718600 | tf_op jit(solution)/shard_map/ppermute | solution.py:19
  285.0 56.8 %copy-start.2 = (bf16[512,768]{1,0:T(8,128)(2,1)S(1)}, bf16[512,768]{1,0:T(8,128)(2,1)}, u32[]{:S(2)}) copy-start(bf16[512,768]{1,0:T(8,128)(2,1)} %param.18) | copy-start | bytes 2359300
  285.0 66.1 %all-gather.8.cloned.1.call-start = ((), (), s32[]{:S(2)}) async-start(), calls=%async_computation.4 | async-start | bytes 3538944 | tf_op jit(solution)/shard_map/all_gather | solution.py:112
  285.6 94.5 %all-gather.4.cloned.1.call-start = ((), (), s32[]{:S(2)}) async-start(), calls=%async_computation.2 | async-start | bytes 3932160 | tf_op jit(solution)/shard_map/all_gather | solution.py:104
  343.5 41.3 %copy-start.1 = (bf16[512,768]{1,0:T(8,128)(2,1)}, bf16[512,768]{1,0:T(8,128)(2,1)S(1)}, u32[]{:S(2)}) copy-start(bf16[512,768]{1,0:T(8,128)(2,1)S(1)} %get-tuple-element.301) | copy-start | bytes 2359300
  350.6 146.4 %all-gather.6.cloned.1.call-start = ((), (), s32[]{:S(2)}) async-start(), calls=%async_computation.3 | async-start | bytes 5308416 | tf_op jit(solution)/shard_map/all_gather | solution.py:107
  384.8 118.3 %collective-permute-start.4 = (bf16[512,512]{1,0:T(8,128)(2,1)S(1)}, bf16[512,512]{1,0:T(8,128)(2,1)}, u32[]{:S(2)}, u32[]{:S(2)}) collective-permute-start(bf16[512,512]{1,0:T(8,128)(2,1)S(1)} %convolution_convert_fusion.1), channel_id=1, source_target_pairs={{0,16},{4,20},{8,24},{12,28},{1,17},{5,21},{9,25},{13,29},{2,18},{... | collective-permute-start | bytes 1572872 | tf_op jit(solution)/shard_map/ppermute | solution.py:19
  386.1 118.1 %collective-permute-start.5 = (bf16[512,512]{1,0:T(8,128)(2,1)S(1)}, bf16[512,512]{1,0:T(8,128)(2,1)}, u32[]{:S(2)}, u32[]{:S(2)}) collective-permute-start(bf16[512,512]{1,0:T(8,128)(2,1)S(1)} %convolution_convert_fusion.1), channel_id=1, source_target_pairs={{0,12},{4,16},{8,20},{12,24},{16,28},{1,13},{5,17},{9,21},{13,25},... | collective-permute-start | bytes 1572872 | tf_op jit(solution)/shard_map/ppermute | solution.py:19
  390.1 115.2 %collective-permute-start.6 = (bf16[512,512]{1,0:T(8,128)(2,1)S(1)}, bf16[512,512]{1,0:T(8,128)(2,1)S(1)}, u32[]{:S(2)}, u32[]{:S(2)}) collective-permute-start(bf16[512,512]{1,0:T(8,128)(2,1)S(1)} %convolution_convert_fusion.1), channel_id=1, source_target_pairs={{0,8},{4,12},{8,16},{12,20},{16,24},{20,28},{1,9},{5,13},{9,17},{1... | collective-permute-start | bytes 1572872 | tf_op jit(solution)/shard_map/ppermute | solution.py:19
  392.0 123.5 %collective-permute-start.7 = (bf16[512,512]{1,0:T(8,128)(2,1)S(1)}, bf16[512,512]{1,0:T(8,128)(2,1)S(1)}, u32[]{:S(2)}, u32[]{:S(2)}) collective-permute-start(bf16[512,512]{1,0:T(8,128)(2,1)S(1)} %convolution_convert_fusion.1), channel_id=1, source_target_pairs={{0,4},{4,8},{8,12},{12,16},{16,20},{20,24},{24,28},{1,5},{5,9},{9,... | collective-permute-start | bytes 1572872 | tf_op jit(solution)/shard_map/ppermute | solution.py:19
Sparse Core Ops, SparseCore 0:
  285.1 56.6 reduce-scatter.1
Sparse Core Ops, SparseCore 1:
  287.7 57.5 all-gather.7
  350.6 29.4 all-gather.3
  382.2 114.7 all-gather.5
where the time goes:
time: 587 us; the launch traced here: 585 us
  waiting for transfers between devices  388 us (66%)
  matrix products  74.1 us (13%)
  loops' own time  35.9 us (6%)
  local copies, waits for them, and re-layouts  31.7 us (5%)
  starting transfers between devices  18.8 us (3%)
  between operations  16.6 us (3%)
  other arithmetic  13.5 us (2%)
  blocking collectives  5.87 us (1%)
    ppermute x8, waiting for transfers between devices, passed_along(): return lax.ppermute(block, axis, route)  200 us
    all_gather x1, waiting for transfers between devices, local(): lax.all_gather(w_query, 'seq', axis=0, tiled=True)  103 us
    reduce_scatter x1, waiting for transfers between devices, local(): lax.psum_scatter(partial_terms, 'head', scatter_dimension=1, tiled=True)  55.4 us
    dot_general x12, matrix products, one_head(): lax.dot_general(query_head, key_head, (((1,), (1,)), ((), ())), preferred...  39.3 us
    another operation x2, loops' own time, attend(): per_head = lax.map(one_head, jnp.arange(head_count, dtype=jnp.int32))  35.9 us
    all_gather x1, waiting for transfers between devices, local(): normed = lax.all_gather(normed_share, 'head', axis=1, tiled=True)  29 us
    ppermute x8, starting transfers between devices, passed_along(): return lax.ppermute(block, axis, route)  18.6 us
    dot_general x12, matrix products, one_head(): jnp.dot(weights.astype(jnp.bfloat16), value_head, preferred_element_type=...  17.4 us
  transfers between devices with their start and end apart: 12, of which 8 were waited for; matrix products, arithmetic and copies ran while one was open for 4% of the time, Pallas kernels for 0%

commit v1 on v0

--- a/solution.py
+++ b/solution.py
@@ -11,6 +11,28 @@
 WIN_BLOCKS = 4
 DOC_BLOCKS = 5
 EPSILON = 1e-06
+
+
+def laid_out(parts, dim):
+    parts = jnp.moveaxis(parts, 0, dim)
+    lengths = parts.shape
+    return parts.reshape(*lengths[:dim], lengths[dim] * lengths[dim + 1], *lengths[dim + 2 :])
+
+
+def grow_blocks(x, axis):
+    peers = lax.axis_size(axis)
+    blocks = x[None]
+    for level in range(peers.bit_length() - 1):
+        bit = 1 << level
+        theirs = lax.ppermute(blocks, axis, [(i, i ^ bit) for i in range(peers)])
+        both = jnp.stack([blocks, theirs])
+        upper = lax.axis_index(axis) >> level & 1
+        blocks = jnp.where(upper == 0, both, both[::-1]).reshape(-1, *x.shape)
+    return blocks
+
+
+def collect(array, axis, dim):
+    return laid_out(grow_blocks(array, axis), dim)
 
 
 def passed_along(block, axis, distance):
@@ -102,11 +124,7 @@
     )
     normed_share = (wide * inverse_rms[:, None] * gain_share).astype(jnp.bfloat16)
     normed = lax.all_gather(normed_share, "head", axis=1, tiled=True)
-    query_sum = jnp.dot(
-        normed,
-        lax.all_gather(w_query, "seq", axis=0, tiled=True),
-        preferred_element_type=jnp.float32,
-    )
+    query_sum = jnp.dot(normed, collect(w_query, "seq", 0), preferred_element_type=jnp.float32)
     cache_sum = jnp.dot(
         normed,
         lax.all_gather(w_cache, "seq", axis=0, tiled=True),

time: 587 us -> 616 us (1.049)
  waiting for transfers between devices: 388 us -> 409 us
  other arithmetic: 13.5 us -> 21.2 us
    ppermute x0 -> x3, waiting for transfers between devices: none -> 125 us  [grow_blocks(): theirs = lax.ppermute(blocks, axis, [(i, i ^ bit) for i in range(peers)])]
    all_gather x1 -> x0, waiting for transfers between devices: 103 us -> none  [local(): lax.all_gather(w_query, 'seq', axis=0, tiled=True)]
    ppermute x8, waiting for transfers between devices: 200 us -> 245 us  [passed_along(): return lax.ppermute(block, axis, route)]
    all_gather x1, waiting for transfers between devices: 29 us -> 0.01 us  [local(): normed = lax.all_gather(normed_share, 'head', axis=1, tiled=True)]
    reduce_scatter x1, waiting for transfers between devices: 55.4 us -> 38 us  [local(): lax.psum_scatter(partial_terms, 'head', scatter_dimension=1, tiled=True)]
    unnamed x21 -> x25, local copies, waits for them, and re-layouts: 15 us -> 15.4 us
  transfers between devices with their start and end apart: 12 -> 14, of which waited for: 8 -> 11; matrix products, arithmetic and copies ran while one was open for 4% -> 4% of each run, Pallas kernels for 0% -> 0%
where the time goes in v1:
time: 616 us; the launch traced here: 614 us
  waiting for transfers between devices  409 us (66%)
  matrix products  71.1 us (12%)
  loops' own time  35.3 us (6%)
  local copies, waits for them, and re-layouts  31.9 us (5%)
  starting transfers between devices  23.1 us (4%)
  other arithmetic  21.2 us (3%)
  between operations  16.5 us (3%)
    ppermute x8, waiting for transfers between devices, passed_along(): return lax.ppermute(block, axis, route)  245 us
    ppermute x3, waiting for transfers between devices, grow_blocks(): theirs = lax.ppermute(blocks, axis, [(i, i ^ bit) for i in range(peers)])  125 us
    dot_general x12, matrix products, one_head(): lax.dot_general(query_head, key_head, (((1,), (1,)), ((), ())), preferred...  39.4 us
    reduce_scatter x1, waiting for transfers between devices, local(): lax.psum_scatter(partial_terms, 'head', scatter_dimension=1, tiled=True)  38 us
    another operation x2, loops' own time, attend(): per_head = lax.map(one_head, jnp.arange(head_count, dtype=jnp.int32))  35.3 us
    ppermute x8, starting transfers between devices, passed_along(): return lax.ppermute(block, axis, route)  22.9 us
    dot_general x12, matrix products, one_head(): jnp.dot(weights.astype(jnp.bfloat16), value_head, preferred_element_type=...  17.4 us
    unnamed x25, local copies, waits for them, and re-layouts  15.4 us
  transfers between devices with their start and end apart: 14, of which 11 were waited for; matrix products, arithmetic and copies ran while one was open for 4% of the time, Pallas kernels for 0%

profile of v1, /device:TPU:17, one launch (start us, length us, event | category | flops | bytes accessed | tf_op | source)
XLA Modules:
  0.0 613.9 jit_solution(6557726302203959275)
XLA Ops:
  8.1 1.4 copy.14
  9.5 1.4 copy.15
  11.0 1.3 collective-permute-start
  12.3 4.2 collective-permute-start.1
  16.5 1.9 collective-permute-start.2
  18.4 1.9 collective-permute-start.3
  23.3 2.3 copy.13
  25.6 23.7 %collective-permute-done = bf16[512,1536]{0,1:T(8,128)(2,1)} collective-permute-done((bf16[512,1536]{0,1:T(8,128)(2,1)S(1)}, bf16[512,1536]{0,1:T(8,128)(2,1)}, u32[]{:S(2)}, u32[]{:S(2)}) %collective-permute-start) | collective-permute-done | bytes 1572896 | tf_op jit(solution)/shard_map/ppermute | solution.py:41
  49.2 1.5 constant_dynamic-update-slice_fusion.6
  50.7 33.1 %collective-permute-done.1 = bf16[512,1536]{0,1:T(8,128)(2,1)} collective-permute-done((bf16[512,1536]{0,1:T(8,128)(2,1)S(1)}, bf16[512,1536]{0,1:T(8,128)(2,1)}, u32[]{:S(2)}, u32[]{:S(2)}) %collective-permute-start.1) | collective-permute-done | bytes 1572896 | tf_op jit(solution)/shard_map/ppermute | solution.py:41
  83.9 1.5 constant_dynamic-update-slice_fusion.5
  85.4 66.0 %collective-permute-done.2 = bf16[512,1536]{0,1:T(8,128)(2,1)} collective-permute-done((bf16[512,1536]{0,1:T(8,128)(2,1)S(1)}, bf16[512,1536]{0,1:T(8,128)(2,1)}, u32[]{:S(2)}, u32[]{:S(2)}) %collective-permute-start.2) | collective-permute-done | bytes 1572896 | tf_op jit(solution)/shard_map/ppermute | solution.py:41
  151.4 1.5 constant_dynamic-update-slice_fusion.4
  152.9 66.9 %collective-permute-done.3 = bf16[512,1536]{0,1:T(8,128)(2,1)} collective-permute-done((bf16[512,1536]{0,1:T(8,128)(2,1)S(1)}, bf16[512,1536]{0,1:T(8,128)(2,1)}, u32[]{:S(2)}, u32[]{:S(2)}) %collective-permute-start.3) | collective-permute-done | bytes 1572896 | tf_op jit(solution)/shard_map/ppermute | solution.py:41
  219.8 1.5 constant_dynamic-update-slice_fusion.3
  221.4 3.4 fusion.62
  224.8 52.4 %while.27 = (s32[]{:T(128)}, bf16[6,512,128]{1,2,0:T(8,128)(2,1)S(1)}, s32[6]{0:T(128)S(1)}, bf16[512,6,128]{0,2,1:T(8,128)(2,1)}, bf16[2560,6,128]{0,2,1:T(8,12...) while((s32[]{:T(128)}, ...), condition=%wide.region_3.6_spmd.clone, body=%wide.region_0.5_spmd.clone.sunk | while | flops 686947328 | bytes 17852076 | solution.py:89
  227.3 3.2 fusion.82
  231.4 2.0 fusion.84
  236.1 3.2 fusion.82
  240.1 2.0 fusion.84
  244.8 3.2 fusion.82
  248.9 2.0 fusion.84
  253.6 3.2 fusion.82
  257.6 2.0 fusion.84
  262.3 3.2 fusion.82
  266.4 2.0 fusion.84
  271.0 3.2 fusion.82
  275.1 2.0 fusion.84
  277.3 6.9 %fusion.63 = f32[512,3072]{1,0:T(8,128)} fusion(bf16[512,768]{0,1:T(8,128)(2,1)S(1)} %bitcast.103, bf16[768,3072]{1,0:T(8,128)(2,1)} %param.22), kind=kOutput, calls=%fused_computation.95 | convolution fusion | flops 2415919104 | bytes 11796480 | tf_op jit(solution)/shard_map/dot_general | solution.py:115
  286.0 16.6 %collective-permute-done.4 = bf16[1,384,768]{2,1,0:T(8,128)(2,1)S(1)} collective-permute-done((bf16[1,384,768]{2,1,0:T(8,128)(2,1)S(1)}, bf16[1,384,768]{2,1,0:T(8,128)(2,1)S(1)}, u32[]{:S(2)}, u32[]{:S(2)}) %collective-permute-start.4) | collective-permute-done | bytes 589856 | tf_op jit(solution)/shard_map/ppermute | solution.py:27
  303.0 38.0 %reduce-scatter.2.cloned.1.call-done = f32[512,768]{1,0:T(8,128)} async-done(((f32[512,3072]{1,0:T(8,128)}), f32[512,768]{1,0:T(8,128)}) %reduce-scatter.2.cloned.1.call-update) | async-done | bytes 1572880 | tf_op jit(solution)/shard_map/reduce_scatter | solution.py:117
  341.0 1.9 fusion.52
  342.9 6.0 psum.7
  348.9 1.1 fusion.54
  350.1 9.4 %collective-permute-done.5 = bf16[2,384,768]{2,1,0:T(8,128)(2,1)} collective-permute-done((bf16[2,384,768]{2,1,0:T(8,128)(2,1)S(1)}, bf16[2,384,768]{2,1,0:T(8,128)(2,1)}, u32[]{:S(2)}, u32[]{:S(2)}) %collective-permute-start.5) | collective-permute-done | bytes 1179680 | tf_op jit(solution)/shard_map/ppermute | solution.py:27
  359.4 1.5 pad_maximum_fusion.1
  361.5 99.5 %collective-permute-done.6 = bf16[4,384,768]{2,1,0:T(8,128)(2,1)} collective-permute-done((bf16[4,384,768]{2,1,0:T(8,128)(2,1)S(1)}, bf16[4,384,768]{2,1,0:T(8,128)(2,1)}, u32[]{:S(2)}, u32[]{:S(2)}) %collective-permute-start.6) | collective-permute-done | bytes 2359328 | tf_op jit(solution)/shard_map/ppermute | solution.py:27
  461.0 2.1 pad_maximum_fusion
  463.1 3.0 reverse_select_fusion
  466.1 4.8 convolution_convert_fusion.1
  470.9 1.3 collective-permute-start.7
  472.2 8.4 %collective-permute-start.8 = (bf16[512,512]{1,0:T(8,128)(2,1)S(1)}, bf16[512,512]{1,0:T(8,128)(2,1)}, u32[]{:S(2)}, u32[]{:S(2)}) collective-permute-start(bf16[512,512]{1,0:T(8,128)(2,1)S(1)} %convolution_convert_fusion.1), channel_id=1, source_target_pairs={{0,12},{4,16},{8,20},{12,24},{16,28},{1,13},{5,17},{9,21},{13,25},... | collective-permute-start | bytes 1572872 | tf_op jit(solution)/shard_map/ppermute | solution.py:41
  480.7 1.9 collective-permute-start.9
  482.6 1.9 collective-permute-start.10
  484.5 2.6 convolution_convert_fusion
  487.5 1.1 constant_dynamic-update-slice_fusion.11
  488.5 14.2 %collective-permute-done.8 = bf16[512,512]{1,0:T(8,128)(2,1)} collective-permute-done((bf16[512,512]{1,0:T(8,128)(2,1)S(1)}, bf16[512,512]{1,0:T(8,128)(2,1)}, u32[]{:S(2)}, u32[]{:S(2)}) %collective-permute-start.8) | collective-permute-done | bytes 524320 | tf_op jit(solution)/shard_map/ppermute | solution.py:41
  502.7 1.1 constant_dynamic-update-slice_fusion.10
  503.8 17.7 %collective-permute-done.9 = bf16[512,512]{1,0:T(8,128)(2,1)S(1)} collective-permute-done((bf16[512,512]{1,0:T(8,128)(2,1)S(1)}, bf16[512,512]{1,0:T(8,128)(2,1)S(1)}, u32[]{:S(2)}, u32[]{:S(2)}) %collective-permute-start.9) | collective-permute-done | bytes 524320 | tf_op jit(solution)/shard_map/ppermute | solution.py:41
  521.6 23.3 %collective-permute-done.10 = bf16[512,512]{1,0:T(8,128)(2,1)S(1)} collective-permute-done((bf16[512,512]{1,0:T(8,128)(2,1)S(1)}, bf16[512,512]{1,0:T(8,128)(2,1)S(1)}, u32[]{:S(2)}, u32[]{:S(2)}) %collective-permute-start.10) | collective-permute-done | bytes 524320 | tf_op jit(solution)/shard_map/ppermute | solution.py:41
  545.5 1.2 copy.39
  546.7 58.6 %while.28 = (s32[]{:T(128)}, bf16[6,512,128]{1,2,0:T(8,128)(2,1)S(1)}, s32[6]{0:T(128)S(1)}, bf16[512,6,128]{0,2,1:T(8,128)(2,1)S(1)}, bf16[2560,2,128]{2,0,1:T(...) while((s32[]{:T(128)}, ...), condition=%wide.region_10.13_spmd.clone, body=%wide.region_7.12_spmd.clone.sunk | while | flops 686947328 | bytes 17853756 | solution.py:89
  551.2 3.4 fusion.87
  555.4 0.9 fusion.89
  561.0 3.4 fusion.87
  565.2 0.9 fusion.89
  570.7 3.4 fusion.87
  574.9 0.9 fusion.89
  580.5 3.4 fusion.87
  590.3 3.4 fusion.87
  594.5 0.9 fusion.89
  600.0 3.4 fusion.87
  605.3 1.2 copy.25
  (106 shorter events, 27.1 us)
Async XLA Ops:
  8.0 12.3 %copy-start = (s32[8]{0:T(128)S(1)}, s32[8]{0:T(128)}, u32[]{:S(2)}) copy-start(s32[8]{0:T(128)} %param.26) | copy-start | bytes 100
  8.0 14.4 %copy-start.4 = (s32[8]{0:T(128)S(1)}, s32[8]{0:T(128)}, u32[]{:S(2)}) copy-start(s32[8]{0:T(128)} %param.27) | copy-start | bytes 100
  8.0 332.9 %reduce-scatter.2.cloned.1.call-start = ((), (), s32[]{:S(2)}) async-start(), calls=%async_computation.1 | async-start | bytes 7864320 | tf_op jit(solution)/shard_map/reduce_scatter | solution.py:117
  11.0 38.2 %collective-permute-start = (bf16[512,1536]{0,1:T(8,128)(2,1)S(1)}, bf16[512,1536]{0,1:T(8,128)(2,1)}, u32[]{:S(2)}, u32[]{:S(2)}) collective-permute-start(bf16[512,1536]{0,1:T(8,128)(2,1)S(1)} %pad_maximum_fusion.2), channel_id=1, source_target_pairs={{0,16},{4,20},{8,24},{12,28},{1,17},{5,21},{9,25},{13,29},{2,18},{... | collective-permute-start | bytes 4718600 | tf_op jit(solution)/shard_map/ppermute | solution.py:41
  12.3 71.6 %collective-permute-start.1 = (bf16[512,1536]{0,1:T(8,128)(2,1)S(1)}, bf16[512,1536]{0,1:T(8,128)(2,1)}, u32[]{:S(2)}, u32[]{:S(2)}) collective-permute-start(bf16[512,1536]{0,1:T(8,128)(2,1)S(1)} %pad_maximum_fusion.2), channel_id=1, source_target_pairs={{0,12},{4,16},{8,20},{12,24},{16,28},{1,13},{5,17},{9,21},{13,25},... | collective-permute-start | bytes 4718600 | tf_op jit(solution)/shard_map/ppermute | solution.py:41
  16.5 134.9 %collective-permute-start.2 = (bf16[512,1536]{0,1:T(8,128)(2,1)S(1)}, bf16[512,1536]{0,1:T(8,128)(2,1)}, u32[]{:S(2)}, u32[]{:S(2)}) collective-permute-start(bf16[512,1536]{0,1:T(8,128)(2,1)S(1)} %pad_maximum_fusion.2), channel_id=1, source_target_pairs={{0,8},{4,12},{8,16},{12,20},{16,24},{20,28},{1,9},{5,13},{9,17},{1... | collective-permute-start | bytes 4718600 | tf_op jit(solution)/shard_map/ppermute | solution.py:41
  18.4 201.3 %collective-permute-start.3 = (bf16[512,1536]{0,1:T(8,128)(2,1)S(1)}, bf16[512,1536]{0,1:T(8,128)(2,1)}, u32[]{:S(2)}, u32[]{:S(2)}) collective-permute-start(bf16[512,1536]{0,1:T(8,128)(2,1)S(1)} %pad_maximum_fusion.2), channel_id=1, source_target_pairs={{0,4},{4,8},{8,12},{12,16},{16,20},{20,24},{24,28},{1,5},{5,9},{9,... | collective-permute-start | bytes 4718600 | tf_op jit(solution)/shard_map/ppermute | solution.py:41
  284.1 1.1 copy-start.3
  284.2 182.0 %all-gather.5.cloned.1.call-start = ((), (), s32[]{:S(2)}) async-start(), calls=%async_computation.3 | async-start | bytes 3538944 | tf_op jit(solution)/shard_map/all_gather | solution.py:130
  284.7 181.4 %all-gather.3.cloned.1.call-start = ((), (), s32[]{:S(2)}) async-start(), calls=%async_computation.2 | async-start | bytes 3932160 | tf_op jit(solution)/shard_map/all_gather | solution.py:126
  285.2 17.3 %collective-permute-start.4 = (bf16[1,384,768]{2,1,0:T(8,128)(2,1)S(1)}, bf16[1,384,768]{2,1,0:T(8,128)(2,1)S(1)}, u32[]{:S(2)}, u32[]{:S(2)}) collective-permute-start(bf16[1,384,768]{2,1,0:T(8,128)(2,1)S(1)} %bitcast.107), channel_id=1, source_target_pairs={{0,4},{4,0},{8,12},{12,8},{16,20},{20,16},{24,28},{28,24},{1,5},{5... | collective-permute-start | bytes 1769480 | tf_op jit(solution)/shard_map/ppermute | solution.py:27
  302.9 56.5 %collective-permute-start.5 = (bf16[2,384,768]{2,1,0:T(8,128)(2,1)S(1)}, bf16[2,384,768]{2,1,0:T(8,128)(2,1)}, u32[]{:S(2)}, u32[]{:S(2)}) collective-permute-start(bf16[2,384,768]{2,1,0:T(8,128)(2,1)S(1)} %get-tuple-element.311), channel_id=1, source_target_pairs={{0,8},{4,12},{8,0},{12,4},{16,24},{20,28},{24,16},{28,20},{1,9},{5... | collective-permute-start | bytes 3538952 | tf_op jit(solution)/shard_map/ppermute | solution.py:27
  342.9 18.1 %copy-start.2 = (bf16[512,768]{1,0:T(8,128)(2,1)}, bf16[512,768]{1,0:T(8,128)(2,1)S(1)}, u32[]{:S(2)}) copy-start(bf16[512,768]{1,0:T(8,128)(2,1)S(1)} %get-tuple-element.301) | copy-start | bytes 2359300
  361.4 99.6 %collective-permute-start.6 = (bf16[4,384,768]{2,1,0:T(8,128)(2,1)S(1)}, bf16[4,384,768]{2,1,0:T(8,128)(2,1)}, u32[]{:S(2)}, u32[]{:S(2)}) collective-permute-start(bf16[4,384,768]{2,1,0:T(8,128)(2,1)S(1)} %bitcast.98), channel_id=1, source_target_pairs={{0,16},{4,20},{8,24},{12,28},{16,0},{20,4},{24,8},{28,12},{1,17},{... | collective-permute-start | bytes 7077896 | tf_op jit(solution)/shard_map/ppermute | solution.py:27
  466.1 18.4 %copy-start.1 = (bf16[2,4,384,768]{3,2,1,0:T(8,128)(2,1)S(1)}, bf16[2,4,384,768]{3,2,1,0:T(8,128)(2,1)}, u32[]{:S(2)}) copy-start(bf16[2,4,384,768]{3,2,1,0:T(8,128)(2,1)} %reverse_select_fusion) | copy-start | bytes 14155780
  466.1 18.4 %copy-start.5 = (bf16[512,3072]{1,0:T(8,128)(2,1)S(1)}, bf16[512,3072]{1,0:T(8,128)(2,1)}, u32[]{:S(2)}) copy-start(bf16[512,3072]{1,0:T(8,128)(2,1)} %all-gather.3.cloned.1.call-done) | copy-start | bytes 9437188
  470.9 16.5 %collective-permute-start.7 = (bf16[512,512]{1,0:T(8,128)(2,1)S(1)}, bf16[512,512]{1,0:T(8,128)(2,1)}, u32[]{:S(2)}, u32[]{:S(2)}) collective-permute-start(bf16[512,512]{1,0:T(8,128)(2,1)S(1)} %convolution_convert_fusion.1), channel_id=1, source_target_pairs={{0,16},{4,20},{8,24},{12,28},{1,17},{5,21},{9,25},{13,29},{2,18},{... | collective-permute-start | bytes 1572872 | tf_op jit(solution)/shard_map/ppermute | solution.py:41
  472.2 30.5 %collective-permute-start.8 = (bf16[512,512]{1,0:T(8,128)(2,1)S(1)}, bf16[512,512]{1,0:T(8,128)(2,1)}, u32[]{:S(2)}, u32[]{:S(2)}) collective-permute-start(bf16[512,512]{1,0:T(8,128)(2,1)S(1)} %convolution_convert_fusion.1), channel_id=1, source_target_pairs={{0,12},{4,16},{8,20},{12,24},{16,28},{1,13},{5,17},{9,21},{13,25},... | collective-permute-start | bytes 1572872 | tf_op jit(solution)/shard_map/ppermute | solution.py:41
  480.7 40.9 %collective-permute-start.9 = (bf16[512,512]{1,0:T(8,128)(2,1)S(1)}, bf16[512,512]{1,0:T(8,128)(2,1)S(1)}, u32[]{:S(2)}, u32[]{:S(2)}) collective-permute-start(bf16[512,512]{1,0:T(8,128)(2,1)S(1)} %convolution_convert_fusion.1), channel_id=1, source_target_pairs={{0,8},{4,12},{8,16},{12,20},{16,24},{20,28},{1,9},{5,13},{9,17},{1... | collective-permute-start | bytes 1572872 | tf_op jit(solution)/shard_map/ppermute | solution.py:41
  482.6 62.3 %collective-permute-start.10 = (bf16[512,512]{1,0:T(8,128)(2,1)S(1)}, bf16[512,512]{1,0:T(8,128)(2,1)S(1)}, u32[]{:S(2)}, u32[]{:S(2)}) collective-permute-start(bf16[512,512]{1,0:T(8,128)(2,1)S(1)} %convolution_convert_fusion.1), channel_id=1, source_target_pairs={{0,4},{4,8},{8,12},{12,16},{16,20},{20,24},{24,28},{1,5},{5,9},{9,... | collective-permute-start | bytes 1572872 | tf_op jit(solution)/shard_map/ppermute | solution.py:41
Sparse Core Ops, SparseCore 0:
  284.3 56.6 reduce-scatter.1
Sparse Core Ops, SparseCore 1:
  286.8 73.4 all-gather.4
  362.3 28.6 all-gather.2
